TPU v7x, 32 devices: a whole 2x2x4 slice. The times are simulated.
32 devices in a mesh: blk: 4 (over z), tok: 8 (over y, x, core).
Axes of the slice: x: 2, y: 2, z: 4, core: 2. Of those that a mesh axis runs over, the one named last changes fastest.
Arguments:
- inputs: float32 [2048, 16384], P('tok', 'blk'), may hold values from -6 to 6
- first_factor: float32 [16, 1024, 1024], P('blk', 'tok'), may hold values from -0.1875 to 0.1875
- second_factor: float32 [16, 1024, 1024], P('blk', 'tok'), may hold values from -0.1875 to 0.1875
- cotangent: float32 [2048, 16384], P('tok', 'blk'), may hold values from -6 to 6
Outputs:
- input_grad: float32 [2048, 16384], P('tok', 'blk')
- first_grad: float32 [16, 1024, 1024], P('blk', 'tok')
- second_grad: float32 [16, 1024, 1024], P('blk', 'tok')
All inputs are finite; a program needn't handle non-finite values.
Results may differ from a plain program's by a relative error of at most 0.00013.
Values sent between devices are 32-bit elements; how exact they have to be, the bound alone decides.
No kernel may reach another device: no remote copies, remote signals or barrier semaphores. Data moves between devices by JAX's collectives and lax.ppermute only.
A program may use at most 128 MiB of HBM per device.

v0:
```python
import math
import jax
import jax.numpy as jnp
from jax import lax
from jax.sharding import PartitionSpec as P


def body(inputs, first_factor, second_factor, cotangent):
    hp = lax.Precision.HIGHEST
    local_blocks = first_factor.shape[0]
    order = first_factor.shape[2]
    blocks = local_blocks * lax.axis_size("blk")
    group = order // blocks
    count = inputs.shape[0]
    xb = inputs.reshape(count, local_blocks, order)
    first_whole, second_whole = (
        lax.all_gather(first_factor, "tok", axis=1, tiled=True),
        lax.all_gather(second_factor, "tok", axis=1, tiled=True),
    )
    first_view = first_whole.reshape(local_blocks, order, blocks, group)
    first = jnp.einsum("tbi,bisg->stbg", xb, first_view, precision=hp).reshape(
        blocks, count, local_blocks * group
    )
    mixed = lax.all_to_all(first, "blk", split_axis=0, concat_axis=2, tiled=True)
    second = jnp.einsum("btk,bko->tbo", mixed, second_whole, precision=hp)
    normal_cdf = 0.5 * (1.0 + jax.scipy.special.erf(second / math.sqrt(2.0)))
    density = jnp.exp(-0.5 * second * second) / math.sqrt(2.0 * math.pi)
    delta_second = cotangent.reshape(count, local_blocks, order) * (normal_cdf + second * density)
    second_grad = jnp.einsum("btk,tbo->bko", mixed, delta_second, precision=hp)
    second_out = lax.psum_scatter(second_grad, "tok", scatter_dimension=1, tiled=True)
    delta_mixed = jnp.einsum("tbo,bko->btk", delta_second, second_whole, precision=hp)
    delta_first = lax.all_to_all(delta_mixed, "blk", split_axis=2, concat_axis=0, tiled=True)
    delta_view = delta_first.reshape(blocks, count, local_blocks, group)
    first_grad = jnp.einsum("tbi,stbg->bisg", xb, delta_view, precision=hp).reshape(
        local_blocks, order, order
    )
    input_grad = jnp.einsum("stbg,bisg->tbi", delta_view, first_view, precision=hp).reshape(
        count, local_blocks * order
    )
    first_out = lax.psum_scatter(first_grad, "tok", scatter_dimension=1, tiled=True)
    return (input_grad, first_out, second_out)


def solution(mesh):
    placed = (P("tok", "blk"), P("blk", "tok", None), P("blk", "tok", None), P("tok", "blk"))
    return jax.shard_map(
        body,
        mesh=mesh,
        in_specs=placed,
        out_specs=(P("tok", "blk"), P("blk", "tok", None), P("blk", "tok", None)),
        check_vma=False,
    )
```

profile of v0, /device:TPU:0, one launch (start us, length us, event | category | flops | bytes accessed | tf_op | source)
XLA Modules:
  0.0 574.6 jit_solution(17563923800015692502)
XLA Ops:
  7.2 0.0 all-gather.3.cloned.1.call-start
  7.2 0.7 all-gather.3.cloned.1.call-update
  7.9 0.0 all-gather.5.cloned.1.call-start
  7.9 0.7 all-gather.5.cloned.1.call-update
  8.6 6.1 %reshape.30 = f32[256,4,1024]{2,1,0:T(4,128)} reshape(f32[256,4096]{1,0:T(8,128)} %param.4) | data formatting | bytes 8388608 | tf_op jit(solution)/shard_map/reshape | solution.py:15
  14.7 87.6 %all-gather.3.cloned.1.call-done = f32[4,1024,1024]{2,1,0:T(8,128)} async-done(((f32[4,128,1024]{2,1,0:T(8,128)}), f32[4,1024,1024]{2,1,0:T(8,128)}) %all-gather.3.cloned.1.call-update) | async-done | bytes 16777232 | tf_op jit(solution)/shard_map/all_gather | solution.py:17
  102.4 16.8 %copy.43 = f32[4,1024,1024]{1,2,0:T(8,128)} copy(f32[4,1024,1024]{2,1,0:T(8,128)} %all-gather.3.cloned.1.call-done) | data formatting | bytes 33554432 | tf_op jit(solution)/shard_map/all_gather | solution.py:17
  119.1 20.6 %fusion.15 = f32[16,256,4,64]{1,3,0,2:T(8,128)S(1)} fusion(f32[4,1024,16,64]{1,3,2,0:T(8,128)} %bitcast.41, f32[256,4,1024,1]{2,1,0,3:T(4,128)} %bitcast.44), kind=kOutput, calls=%fused_computation.17 | convolution fusion | flops 12884901888 | bytes 25165824 | tf_op jit(solution)/shard_map/tbi,bisg->stbg/dot_general | solution.py:21
  139.7 2.4 copy.45
  142.2 5.2 all-to-all-start
  147.4 0.5 reduce-scatter.5.cloned.1.call-start
  147.9 5.6 copy.42
  153.5 5.4 copy.48
  158.9 82.3 %all-to-all-done = f32[16,256,256]{1,2,0:T(8,128)} async-done(((f32[16,256,256]{1,2,0:T(8,128)}), f32[16,256,256]{1,2,0:T(8,128)}, u32[]{:S(2)}, u32[]{:S(2)}) %all-to-all-start) | async-done | bytes 4194336 | tf_op jit(solution)/shard_map/all_to_all | solution.py:24
  241.2 5.2 copy.47
  246.4 5.8 %all_to_all.27 = f32[4,256,1024]{2,1,0:T(8,128)} reshape(f32[4,256,4,256]{3,2,1,0:T(4,128)} %copy.47) | data formatting | bytes 8388608 | tf_op jit(solution)/shard_map/all_to_all | solution.py:24
  252.2 21.3 %fusion.6 = f32[256,4,1024]{2,0,1:T(8,128)S(1)} fusion(f32[256,4,1024]{2,0,1:T(8,128)} %copy.48, f32[4,256,1024]{2,1,0:T(8,128)} %all_to_all.27, f32[4,1024,1024]{2,1,0:T(8,128)} %all-gather.5.cloned.1.call-done), kind=kOutput, calls=%fused_computation.7 | convolution fusion | flops 12894339072 | bytes 29360128 | tf_op jit(solution)/shard_map/btk,bko->tbo/dot_general | solution.py:25
  273.5 2.0 copy-done
  275.5 16.5 %fusion.22 = f32[4,1024,1024]{2,1,0:T(8,128)} fusion(f32[4,256,1024]{2,1,0:T(8,128)S(1)} %copy-done.1, f32[256,4,1024]{2,0,1:T(8,128)S(1)} %fusion.6), kind=kOutput, calls=%fused_computation.20 | convolution fusion | flops 12884901888 | bytes 25165824 | tf_op jit(solution)/shard_map/btk,tbo->bko/dot_general | solution.py:29
  292.1 0.0 reduce-scatter.3.cloned.1.call-start
  292.2 20.2 %fusion.21 = f32[4,256,1024]{2,1,0:T(8,128)} fusion(f32[256,4,1024]{2,0,1:T(8,128)} %copy-done, f32[4,1024,1024]{2,1,0:T(8,128)} %all-gather.5.cloned.1.call-done), kind=kOutput, calls=%fused_computation.19 | convolution fusion | flops 12884901888 | bytes 25165824 | tf_op jit(solution)/shard_map/tbo,bko->btk/dot_general | solution.py:31
  312.3 5.7 copy.49
  318.0 96.6 %all_to_all.33 = f32[4,256,1024]{1,0,2:T(4,128)S(1)} all-to-all(f32[4,256,1024]{1,0,2:T(4,128)} %copy.49), channel_id=1, replica_groups=mesh['blk'=4,'tok'=8] {'blk'}, dimensions={2} | all-to-all | bytes 8388608 | tf_op jit(solution)/shard_map/all_to_all | solution.py:32
  414.6 0.8 copy.50
  415.4 0.4 copy.51
  415.8 3.3 copy-done.2
  419.1 17.7 %fusion.10 = f32[4,16,64,1024]{3,2,1,0:T(8,128)} fusion(f32[16,256,4,64]{1,3,2,0:T(8,128)S(1)} %bitcast.50, f32[256,4,1024,1]{2,1,0,3:T(4,128)S(1)} %bitcast.45), kind=kOutput, calls=%fused_computation.12 | convolution fusion | flops 12884901888 | bytes 25165824 | tf_op jit(solution)/shard_map/tbi,stbg->bisg/dot_general | solution.py:34
  436.8 16.4 %copy.56 = f32[4,1024,1024]{2,1,0:T(8,128)} copy(f32[4,1024,1024]{1,2,0:T(8,128)} %bitcast.43) | data formatting | bytes 33554432 | tf_op jit(solution)/shard_map/reshape | solution.py:34
  453.3 20.1 %fusion.18 = f32[256,4,1024]{2,0,1:T(8,128)} fusion(f32[16,256,4,64]{1,3,2,0:T(8,128)} %bitcast.51, f32[4,1024,16,64]{1,3,2,0:T(8,128)} %bitcast.42), kind=kOutput, calls=%fused_computation.18 | convolution fusion | flops 12884901888 | bytes 25165824 | tf_op jit(solution)/shard_map/stbg,bisg->tbi/dot_general | solution.py:37
  473.3 6.0 %copy.53 = f32[256,4,1024]{0,2,1:T(8,128)} copy(f32[256,4,1024]{2,0,1:T(8,128)} %fusion.18) | data formatting | bytes 8388608 | tf_op jit(solution)/shard_map/stbg,bisg->tbi/transpose | solution.py:37
  479.3 5.7 copy.58
  485.0 82.9 %reduce-scatter.3.cloned.1.call-done = f32[4,128,1024]{2,1,0:T(8,128)} async-done(((f32[4,1024,1024]{2,1,0:T(8,128)}), f32[4,128,1024]{2,1,0:T(8,128)}) %reduce-scatter.3.cloned.1.call-update) | async-done | bytes 2097168 | tf_op jit(solution)/shard_map/reduce_scatter | solution.py:40
  (10 shorter events, 0.1 us)
Async XLA Ops:
  7.2 95.2 %all-gather.3.cloned.1.call-start = ((), (), s32[]{:S(2)}) async-start(), calls=%async_computation.4 | async-start | bytes 18874368 | tf_op jit(solution)/shard_map/all_gather | solution.py:17
  7.9 244.3 %all-gather.5.cloned.1.call-start = ((), (), s32[]{:S(2)}) async-start(), calls=%async_computation.5 | async-start | bytes 18874368 | tf_op jit(solution)/shard_map/all_gather | solution.py:18
  142.2 99.0 %all-to-all-start = ((f32[16,256,256]{1,2,0:T(8,128)}), f32[16,256,256]{1,2,0:T(8,128)}, u32[]{:S(2)}, u32[]{:S(2)}) async-start(f32[16,256,256]{1,2,0:T(8,128)} %bitcast.46), calls=%async_computation | async-start | bytes 8388608 | tf_op jit(solution)/shard_map/all_to_all | solution.py:24
  147.4 337.6 %reduce-scatter.5.cloned.1.call-start = ((), (), s32[]{:S(2)}) async-start(), calls=%async_computation.7 | async-start | bytes 18874368 | tf_op jit(solution)/shard_map/reduce_scatter | solution.py:30
  252.2 23.3 %copy-start.1 = (f32[4,256,1024]{2,1,0:T(8,128)S(1)}, f32[4,256,1024]{2,1,0:T(8,128)}, u32[]{:S(2)}) copy-start(f32[4,256,1024]{2,1,0:T(8,128)} %all_to_all.27) | copy-start | bytes 12582916
  273.5 2.0 copy-start
  292.1 275.7 %reduce-scatter.3.cloned.1.call-start = ((), (), s32[]{:S(2)}) async-start(), calls=%async_computation.6 | async-start | bytes 18874368 | tf_op jit(solution)/shard_map/reduce_scatter | solution.py:40
  415.4 3.7 copy-start.2
  415.8 21.0 %copy-start.3 = (f32[4,4,256,256]{2,3,1,0:T(8,128)}, f32[4,4,256,256]{2,3,1,0:T(8,128)S(1)}, u32[]{:S(2)}) copy-start(f32[4,4,256,256]{2,3,1,0:T(8,128)S(1)} %copy.51) | copy-start | bytes 12582916
Sparse Core Ops, SparseCore 0:
  9.9 92.4 all-gather.2
  104.3 89.7 all-gather.4
  292.2 114.3 reduce-scatter.4
  453.4 114.4 reduce-scatter.2
where the time goes:
time: 581 us; the launch traced here: 575 us
  waiting for transfers between devices  254 us (44%)
  matrix products  116 us (20%)
  blocking collectives  96.6 us (17%)
  local copies, waits for them, and re-layouts  87.6 us (15%)
  between operations  14.1 us (2%)
    all_to_all x1, blocking collectives, body(): lax.all_to_all(delta_mixed, 'blk', split_axis=2, concat_axis=0, tiled=True)  96.6 us
    all_gather x1, waiting for transfers between devices, body(): lax.all_gather(first_factor, 'tok', axis=1, tiled=True)  87.6 us
    reduce_scatter x1, waiting for transfers between devices, body(): lax.psum_scatter(first_grad, 'tok', scatter_dimension=1, tiled=True)  82.9 us
    all_to_all x1, waiting for transfers between devices, body(): lax.all_to_all(first, 'blk', split_axis=0, concat_axis=2, tiled=True)  82.3 us
    dot_general x1, matrix products, body(): second = jnp.einsum('btk,bko->tbo', mixed, second_whole, precision=hp)  21.3 us
    dot_general x1, matrix products, body(): jnp.einsum('tbi,bisg->stbg', xb, first_view, precision=hp)  20.6 us
    dot_general x1, matrix products, body(): jnp.einsum('tbo,bko->btk', delta_second, second_whole, precision=hp)  20.2 us
    dot_general x1, matrix products, body(): jnp.einsum('stbg,bisg->tbi', delta_view, first_view, precision=hp)  20.1 us
  transfers between devices with their start and end apart: 5, of which 3 were waited for; matrix products, arithmetic and copies ran while one was open for 27% of the time, Pallas kernels for 0%

commit v1 on v0

--- a/solution.py
+++ b/solution.py
@@ -3,6 +3,11 @@
 import jax.numpy as jnp
 from jax import lax
 from jax.sharding import PartitionSpec as P
+
+
+def exchange_gather(shard, mesh_axis, along):
+    sent = jnp.stack([shard] * lax.axis_size(mesh_axis))
+    return jnp.concatenate(lax.all_to_all(sent, mesh_axis, 0, 0), axis=along)
 
 
 def body(inputs, first_factor, second_factor, cotangent):
@@ -14,7 +19,7 @@
     count = inputs.shape[0]
     xb = inputs.reshape(count, local_blocks, order)
     first_whole, second_whole = (
-        lax.all_gather(first_factor, "tok", axis=1, tiled=True),
+        exchange_gather(first_factor, "tok", 1),
         lax.all_gather(second_factor, "tok", axis=1, tiled=True),
     )
     first_view = first_whole.reshape(local_blocks, order, blocks, group)

time: 581 us -> 772 us (1.33)
  waiting for transfers between devices: 254 us -> 408 us
  local copies, waits for them, and re-layouts: 87.6 us -> 117 us
    all_to_all x0 -> x1, waiting for transfers between devices: none -> 243 us  [exchange_gather(): return jnp.concatenate(lax.all_to_all(sent, mesh_axis, 0, 0), axis=along)]
    all_gather x1 -> x0, waiting for transfers between devices: 87.6 us -> none  [body(): lax.all_gather(first_factor, 'tok', axis=1, tiled=True)]
    another operation x0 -> x2, local copies, waits for them, and re-layouts: none -> 25.6 us  [the longest x1 18 us: body(): first_view = first_whole.reshape(local_blocks, order, blocks, group)]
    reshape x0 -> x1, local copies, waits for them, and re-layouts: none -> 17.7 us  [exchange_gather(): return jnp.concatenate(lax.all_to_all(sent, mesh_axis, 0, 0), axis=along)]
    all_gather x1 -> x0, local copies, waits for them, and re-layouts: 16.8 us -> none  [body(): lax.all_gather(first_factor, 'tok', axis=1, tiled=True)]
    unnamed x10 -> x11, local copies, waits for them, and re-layouts: 16.6 us -> 18.8 us
  transfers between devices with their start and end apart: 5 -> 5, of which waited for: 3 -> 3; matrix products, arithmetic and copies ran while one was open for 27% -> 24% of each run, Pallas kernels for 0% -> 0%
where the time goes in v1:
time: 772 us; the launch traced here: 762 us
  waiting for transfers between devices  408 us (53%)
  local copies, waits for them, and re-layouts  117 us (15%)
  matrix products  116 us (15%)
  blocking collectives  96.8 us (13%)
  between operations  14.1 us (2%)
  starting transfers between devices  11.6 us (2%)
    all_to_all x1, waiting for transfers between devices, exchange_gather(): return jnp.concatenate(lax.all_to_all(sent, mesh_axis, 0, 0), axis=along)  243 us
    all_to_all x1, blocking collectives, body(): lax.all_to_all(delta_mixed, 'blk', split_axis=2, concat_axis=0, tiled=True)  96.8 us
    reduce_scatter x1, waiting for transfers between devices, body(): lax.psum_scatter(first_grad, 'tok', scatter_dimension=1, tiled=True)  85.2 us
    all_to_all x1, waiting for transfers between devices, body(): lax.all_to_all(first, 'blk', split_axis=0, concat_axis=2, tiled=True)  79.1 us
    dot_general x1, matrix products, body(): second = jnp.einsum('btk,bko->tbo', mixed, second_whole, precision=hp)  21.2 us
    dot_general x1, matrix products, body(): jnp.einsum('tbi,bisg->stbg', xb, first_view, precision=hp)  20.6 us
    dot_general x1, matrix products, body(): jnp.einsum('stbg,bisg->tbi', delta_view, first_view, precision=hp)  19.8 us
    dot_general x1, matrix products, body(): jnp.einsum('tbo,bko->btk', delta_second, second_whole, precision=hp)  19.8 us
  transfers between devices with their start and end apart: 5, of which 3 were waited for; matrix products, arithmetic and copies ran while one was open for 24% of the time, Pallas kernels for 0%

profile of v1, /device:TPU:0, one launch (start us, length us, event | category | flops | bytes accessed | tf_op | source)
XLA Modules:
  0.0 762.4 jit_solution(14009154621496126066)
XLA Ops:
  7.2 0.7 all-gather.2.cloned.1.call-update
  7.9 1.9 copy.44
  9.8 7.6 stack.2
  17.4 6.1 all-to-all-start
  23.6 6.3 reshape.32
  29.9 242.7 %all-to-all-done = f32[8,4,128,1024]{2,3,1,0:T(8,128)} async-done(((f32[8,4,128,1024]{2,3,1,0:T(8,128)}), f32[8,4,128,1024]{2,3,1,0:T(8,128)}, u32[]{:S(2)}, u32[]{:S(2)}) %all-to-all-start) | async-done | bytes 16777248 | tf_op jit(solution)/shard_map/all_to_all | solution.py:10
  272.6 17.7 %copy.45 = f32[4,8,128,1024]{2,1,3,0:T(8,128)} copy(f32[4,8,128,1024]{2,3,0,1:T(8,128)} %bitcast.1) | data formatting | bytes 33554432 | tf_op jit(solution)/shard_map/reshape | solution.py:10
  290.2 18.0 %reshape_reshape.3 = f32[4,1024,16,64]{1,3,2,0:T(8,128)} reshape(f32[4,8,128,1024]{2,1,3,0:T(8,128)} %copy.45) | data formatting | bytes 33554432 | tf_op jit(solution)/shard_map/reshape;reshape | solution.py:25
  308.2 20.6 %fusion.15 = f32[16,256,4,64]{1,3,0,2:T(8,128)S(1)} fusion(f32[4,1024,16,64]{1,3,2,0:T(8,128)} %reshape_reshape.3, f32[256,4,1024,1]{2,1,0,3:T(4,128)} %bitcast.46), kind=kOutput, calls=%fused_computation.17 | convolution fusion | flops 12884901888 | bytes 25165824 | tf_op jit(solution)/shard_map/tbi,bisg->stbg/dot_general | solution.py:26
  328.8 2.4 copy.47
  331.3 4.8 all-to-all-start.1
  336.1 0.5 reduce-scatter.5.cloned.1.call-start
  336.6 5.6 copy.43
  342.2 5.4 copy.50
  347.7 79.1 %all-to-all-done.1 = f32[16,256,256]{1,2,0:T(8,128)} async-done(((f32[16,256,256]{1,2,0:T(8,128)}), f32[16,256,256]{1,2,0:T(8,128)}, u32[]{:S(2)}, u32[]{:S(2)}) %all-to-all-start.1) | async-done | bytes 4194336 | tf_op jit(solution)/shard_map/all_to_all | solution.py:29
  426.8 5.2 copy.49
  432.0 5.8 all_to_all.31
  437.8 21.2 %fusion.6 = f32[256,4,1024]{2,0,1:T(8,128)S(1)} fusion(f32[256,4,1024]{2,0,1:T(8,128)} %copy.50, f32[4,256,1024]{2,1,0:T(8,128)} %all_to_all.31, f32[4,1024,1024]{2,1,0:T(8,128)} %all-gather.2.cloned.1.call-done), kind=kOutput, calls=%fused_computation.7 | convolution fusion | flops 12894339072 | bytes 29360128 | tf_op jit(solution)/shard_map/btk,bko->tbo/dot_general | solution.py:30
  459.0 2.0 copy-done
  461.1 16.6 %fusion.22 = f32[4,1024,1024]{2,1,0:T(8,128)} fusion(f32[4,256,1024]{2,1,0:T(8,128)S(1)} %copy-done.1, f32[256,4,1024]{2,0,1:T(8,128)S(1)} %fusion.6), kind=kOutput, calls=%fused_computation.20 | convolution fusion | flops 12884901888 | bytes 25165824 | tf_op jit(solution)/shard_map/btk,tbo->bko/dot_general | solution.py:34
  477.7 19.8 %fusion.21 = f32[4,256,1024]{2,1,0:T(8,128)} fusion(f32[256,4,1024]{2,0,1:T(8,128)} %copy-done, f32[4,1024,1024]{2,1,0:T(8,128)} %all-gather.2.cloned.1.call-done), kind=kOutput, calls=%fused_computation.19 | convolution fusion | flops 12884901888 | bytes 25165824 | tf_op jit(solution)/shard_map/tbo,bko->btk/dot_general | solution.py:36
  497.5 5.8 copy.51
  503.2 96.8 %all_to_all.38 = f32[4,256,1024]{1,0,2:T(4,128)S(1)} all-to-all(f32[4,256,1024]{1,0,2:T(4,128)} %copy.51), channel_id=1, replica_groups=mesh['blk'=4,'tok'=8] {'blk'}, dimensions={2} | all-to-all | bytes 8388608 | tf_op jit(solution)/shard_map/all_to_all | solution.py:37
  600.0 0.8 copy.52
  600.9 0.4 copy.53
  601.3 3.3 copy-done.2
  604.6 17.7 %fusion.10 = f32[4,16,64,1024]{3,2,1,0:T(8,128)} fusion(f32[16,256,4,64]{1,3,2,0:T(8,128)S(1)} %bitcast.52, f32[256,4,1024,1]{2,1,0,3:T(4,128)S(1)} %bitcast.47), kind=kOutput, calls=%fused_computation.12 | convolution fusion | flops 12884901888 | bytes 25165824 | tf_op jit(solution)/shard_map/tbi,stbg->bisg/dot_general | solution.py:39
  622.3 16.4 %copy.58 = f32[4,1024,1024]{2,1,0:T(8,128)} copy(f32[4,1024,1024]{1,2,0:T(8,128)} %bitcast.45) | data formatting | bytes 33554432 | tf_op jit(solution)/shard_map/reshape | solution.py:39
  638.7 19.8 %fusion.18 = f32[256,4,1024]{2,0,1:T(8,128)} fusion(f32[16,256,4,64]{1,3,2,0:T(8,128)} %bitcast.53, f32[4,1024,16,64]{1,3,2,0:T(8,128)} %reshape_reshape.3), kind=kOutput, calls=%fused_computation.18 | convolution fusion | flops 12884901888 | bytes 25165824 | tf_op jit(solution)/shard_map/stbg,bisg->tbi/dot_general | solution.py:42
  658.5 6.0 copy.55
  664.5 5.9 copy.60
  670.4 85.2 %reduce-scatter.3.cloned.1.call-done = f32[4,128,1024]{2,1,0:T(8,128)} async-done(((f32[4,1024,1024]{2,1,0:T(8,128)}), f32[4,128,1024]{2,1,0:T(8,128)}) %reduce-scatter.3.cloned.1.call-update) | async-done | bytes 2097168 | tf_op jit(solution)/shard_map/reduce_scatter | solution.py:45
  (12 shorter events, 0.1 us)
Async XLA Ops:
  7.2 430.6 %all-gather.2.cloned.1.call-start = ((), (), s32[]{:S(2)}) async-start(), calls=%async_computation.5 | async-start | bytes 18874368 | tf_op jit(solution)/shard_map/all_gather | solution.py:23
  17.4 255.1 %all-to-all-start = ((f32[8,4,128,1024]{2,3,1,0:T(8,128)}), f32[8,4,128,1024]{2,3,1,0:T(8,128)}, u32[]{:S(2)}, u32[]{:S(2)}) async-start(f32[8,4,128,1024]{2,3,1,0:T(8,128)} %stack.2), calls=%async_computation | async-start | bytes 33554432 | tf_op jit(solution)/shard_map/all_to_all | solution.py:10
  331.3 95.5 %all-to-all-start.1 = ((f32[16,256,256]{1,2,0:T(8,128)}), f32[16,256,256]{1,2,0:T(8,128)}, u32[]{:S(2)}, u32[]{:S(2)}) async-start(f32[16,256,256]{1,2,0:T(8,128)} %bitcast.48), calls=%async_computation.1 | async-start | bytes 8388608 | tf_op jit(solution)/shard_map/all_to_all | solution.py:29
  336.1 334.3 %reduce-scatter.5.cloned.1.call-start = ((), (), s32[]{:S(2)}) async-start(), calls=%async_computation.7 | async-start | bytes 18874368 | tf_op jit(solution)/shard_map/reduce_scatter | solution.py:35
  437.8 23.3 %copy-start.1 = (f32[4,256,1024]{2,1,0:T(8,128)S(1)}, f32[4,256,1024]{2,1,0:T(8,128)}, u32[]{:S(2)}) copy-start(f32[4,256,1024]{2,1,0:T(8,128)} %all_to_all.31) | copy-start | bytes 12582916
  459.0 2.0 copy-start
  477.6 278.0 %reduce-scatter.3.cloned.1.call-start = ((), (), s32[]{:S(2)}) async-start(), calls=%async_computation.6 | async-start | bytes 18874368 | tf_op jit(solution)/shard_map/reduce_scatter | solution.py:45
  600.9 3.7 copy-start.2
  601.3 21.0 %copy-start.3 = (f32[4,4,256,256]{2,3,1,0:T(8,128)}, f32[4,4,256,256]{2,3,1,0:T(8,128)S(1)}, u32[]{:S(2)}) copy-start(f32[4,4,256,256]{2,3,1,0:T(8,128)S(1)} %copy.53) | copy-start | bytes 12582916
Sparse Core Ops, SparseCore 0:
  9.9 219.6 all-gather.1
  477.8 116.8 reduce-scatter.4
  638.8 116.7 reduce-scatter.2
